TPU v7x, 32 devices: a whole 2x2x4 slice. The times are simulated.
32 devices in a mesh: row: 8 (over y, x, core), col: 4 (over z).
Axes of the slice: x: 2, y: 2, z: 4, core: 2. Of those that a mesh axis runs over, the one named last changes fastest.
Arguments:
- queries: bfloat16 [8, 128, 4096], P(None, 'row', 'col'), may hold values from -13 to 13, as said below
- key_cache: bfloat16 [8, 16384, 1024], P(None, ('row', 'col')), may hold values from -13 to 13
- value_cache: bfloat16 [8, 16384, 1024], P(None, ('row', 'col')), may hold values from -6 to 6
- key_table: bfloat16 [1024, 1024], replicated, may hold values from -24 to 24
- value_table: bfloat16 [1024, 1024], replicated, may hold values from -6 to 6
- lengths: int32 [8], replicated, may hold values from 2048 to 16384
- token_ids: int32 [8, 128], P(None, 'row'), may hold values from 0 to 1023
Outputs:
- attended: bfloat16 [8, 128, 4096], P(None, 'row', 'col')
Inputs may be any that keep to these rules, and one draw needn't show every extreme that they name: `queries`: entries of the query array lie in the stated range.
All inputs are finite; a program needn't handle non-finite values.
Results may differ from a plain program's by a relative error of at most 0.006.
Values may be sent and summed in bfloat16 or wider, within the bound.
A program may use at most 192 MiB of HBM per device.

v0:
```python
import jax
import jax.numpy as jnp
from jax import lax
from jax.sharding import PartitionSpec as P

HQ = 32
KH = 8
HD = 128


def cache_partials(whole, key_cache, value_cache, lengths, offset):
    users, beams, width = whole.shape
    positions = key_cache.shape[1]
    group = HQ // KH
    scale = HD ** (-0.5)

    def one_user(items):
        q_user, k_user, v_user, limit = items
        q_heads = q_user.reshape(beams, KH, group, HD)
        k_heads = k_user.reshape(positions, KH, HD)
        v_heads = v_user.reshape(positions, KH, HD)
        s = (
            jnp.einsum("wkgd,lkd->kwgl", q_heads, k_heads, preferred_element_type=jnp.float32)
            * scale
        )
        live = offset + jnp.arange(positions, dtype=jnp.int32) < limit
        s = jnp.where(live, s, -1e30)
        peak = jnp.max(s, axis=-1)
        weight = jnp.where(live, jnp.exp(s - peak[..., None]), 0.0)
        total = jnp.sum(weight, axis=-1)
        numer = jnp.einsum(
            "kwgl,lkd->wkgd",
            weight.astype(jnp.bfloat16),
            v_heads,
            preferred_element_type=jnp.float32,
        )
        peak = jnp.transpose(peak, (1, 0, 2)).reshape(beams, HQ)
        total = jnp.transpose(total, (1, 0, 2)).reshape(beams, HQ)
        return (numer.reshape(beams, width), peak, total)

    return lax.map(one_user, (whole, key_cache, value_cache, lengths))


def body(queries, key_cache, value_cache, key_table, value_table, lengths, token_ids):
    users, beam_part, width_part = queries.shape
    heads_part = width_part // HD
    scale = HD ** (-0.5)
    row_at = lax.axis_index("row")
    col_at = lax.axis_index("col")
    whole = lax.all_gather(queries, "col", axis=2, tiled=True)
    whole = lax.all_gather(whole, "row", axis=1, tiled=True)
    offset = (row_at * lax.axis_size("col") + col_at) * key_cache.shape[1]
    numer_part, peak_part, total_part = cache_partials(
        whole, key_cache, value_cache, lengths, offset
    )
    peak_all = lax.pmax(peak_part, ("row", "col"))
    factor = jnp.exp(peak_part - peak_all)
    weighted = (numer_part.reshape(users, -1, HQ, HD) * factor[..., None]).reshape(
        users, -1, HQ * HD
    )
    mass = total_part * factor

    def local_part(array, per_head):
        picked = lax.dynamic_slice_in_dim(array, row_at * beam_part, beam_part, 1)
        return lax.dynamic_slice_in_dim(
            picked, col_at * heads_part * per_head, heads_part * per_head, 2
        )

    numer, total = lax.psum((weighted, mass), ("row", "col"))
    numer = local_part(numer, HD)
    total = local_part(total, 1)
    peak = local_part(peak_all, 1)
    codes = jnp.arange(key_table.shape[0], dtype=jnp.int32)
    onehot = (token_ids[..., None] == codes).astype(jnp.bfloat16)
    own_keys = jnp.einsum("uwv,vc->uwc", onehot, key_table, preferred_element_type=jnp.float32)
    own_values = jnp.einsum("uwv,vc->uwc", onehot, value_table, preferred_element_type=jnp.float32)
    group = HQ // KH
    own_keys = jnp.repeat(own_keys.reshape(users, beam_part, KH, HD), group, axis=2)
    own_values = jnp.repeat(own_values.reshape(users, beam_part, KH, HD), group, axis=2)
    own_keys = lax.dynamic_slice_in_dim(own_keys, col_at * heads_part, heads_part, 2)
    own_values = lax.dynamic_slice_in_dim(own_values, col_at * heads_part, heads_part, 2)
    q_local = queries.astype(jnp.float32).reshape(users, beam_part, heads_part, HD)
    own_score = jnp.sum(q_local * own_keys, axis=-1) * scale
    final_peak = jnp.maximum(peak, own_score)
    carried = jnp.exp(peak - final_peak)
    fresh = jnp.exp(own_score - final_peak)
    numer = (
        numer.reshape(users, beam_part, heads_part, HD) * carried[..., None]
        + fresh[..., None] * own_values
    )
    total = total * carried + fresh
    result = numer / total[..., None]
    return result.reshape(users, beam_part, width_part).astype(jnp.bfloat16)


def solution(mesh):
    return jax.shard_map(
        body,
        mesh=mesh,
        in_specs=(
            P(None, "row", "col"),
            P(None, ("row", "col"), None),
            P(None, ("row", "col"), None),
            P(),
            P(),
            P(),
            P(None, "row"),
        ),
        out_specs=P(None, "row", "col"),
        check_vma=False,
    )
```

profile of v0, /device:TPU:0, one launch (start us, length us, event | category | flops | bytes accessed | tf_op | source)
XLA Modules:
  0.0 730.9 jit_solution(4568035272929321944)
XLA Ops:
  8.6 31.1 %all-gather.3.cloned.1.call-done = bf16[8,16,4096]{2,0,1:T(8,128)(2,1)} async-done(((bf16[8,16,1024]{2,0,1:T(8,128)(2,1)}), bf16[8,16,4096]{2,0,1:T(8,128)(2,1)}) %all-gather.3.cloned.1.call-update) | async-done | bytes 1048592 | tf_op jit(solution)/shard_map/all_gather | solution.py:50
  39.8 55.4 %all-gather.5.cloned.1.call-done = bf16[8,128,4096]{2,0,1:T(8,128)(2,1)} async-done(((bf16[8,16,4096]{2,0,1:T(8,128)(2,1)}), bf16[8,128,4096]{2,0,1:T(8,128)(2,1)}) %all-gather.5.cloned.1.call-update) | async-done | bytes 8388624 | tf_op jit(solution)/shard_map/all_gather | solution.py:51
  95.2 12.5 %copy.37 = bf16[8,128,4096]{1,2,0:T(8,128)(2,1)} copy(bf16[8,128,4096]{2,0,1:T(8,128)(2,1)} %all-gather.5.cloned.1.call-done) | data formatting | bytes 16777216 | tf_op jit(solution)/shard_map/while | solution.py:41
  107.7 186.9 %while.14 = (s32[]{:T(128)}, f32[8,128,4096]{1,2,0:T(8,128)}, f32[8,128,32]{1,2,0:T(8,128)}, f32[8,128,32]{1,2,0:T(8,128)S(1)}, bf16[8,512,1024]{2,1,0:T(8,128)(...) while((s32[]{:T(128)}, f32[8,128,4096]{1,2,0:T(8,128)}, ...), condition=%wide.region_3.4_spmd, body=%wide.region_0.3_spmd.sunk | while | flops 1100997632 | bytes 78777504 | solution.py:41
  112.9 2.8 fusion.35
  115.8 3.2 copy-done.1
  124.6 5.0 fusion.36
  136.3 2.8 fusion.35
  139.1 3.2 copy-done.1
  148.0 5.0 fusion.36
  159.6 2.8 fusion.35
  162.5 3.2 copy-done.1
  171.3 5.0 fusion.36
  183.0 2.8 fusion.35
  185.8 3.2 copy-done.1
  194.7 5.0 fusion.36
  206.4 2.8 fusion.35
  209.2 3.2 copy-done.1
  218.1 5.0 fusion.36
  229.7 2.8 fusion.35
  232.6 3.2 copy-done.1
  241.4 5.0 fusion.36
  253.1 2.8 fusion.35
  256.0 3.2 copy-done.1
  264.8 5.0 fusion.36
  276.5 2.8 fusion.35
  279.3 3.2 copy-done.1
  288.2 5.0 fusion.36
  294.7 124.8 %all-reduce.4.cloned.1.call-done = f32[8,128,32]{1,2,0:T(8,128)} async-done(((f32[8,128,32]{1,2,0:T(8,128)}), f32[8,128,32]{1,2,0:T(8,128)}) %all-reduce.4.cloned.1.call-update) | async-done | bytes 131088 | tf_op jit(solution)/shard_map/pmax | solution.py:56
  421.1 11.3 %bitcast_multiply_fusion = f32[8,128,4096]{1,2,0:T(8,128)} fusion(f32[8,128,4096]{1,2,0:T(8,128)} %get-tuple-element.54, f32[8,128,32]{1,2,0:T(8,128)S(1)} %get-tuple-element.117), kind=kLoop, calls=%fused_computation.17 | loop fusion | flops 4194304 | bytes 33685504 | tf_op jit(solution)/shard_map/mul | solution.py:58
  436.8 276.3 %all-reduce.6.cloned.1.call-done = (f32[8,128,4096]{1,2,0:T(8,128)}, f32[8,128,32]{1,2,0:T(8,128)}) async-done(((f32[8,128,4096]{1,2,0:T(8,128)}, f32[8,128,32]{1,2,0:T(8,128)}), (f32[8,128,4096]{1,2,0:T(8,128)}, f32[8,128,32]{1,2,0:T(8,128)})) %all-reduce.6.cloned.1.call-update) | async-done | bytes 16908304 | tf_op jit(solution)/shard_map/psum | solution.py:69
  714.4 5.3 constant_dynamic-slice_fusion.3
  (125 shorter events, 112.4 us)
Async XLA Ops:
  6.5 425.9 %copy-start = (bf16[1024,1024]{1,0:T(8,128)(2,1)S(1)}, bf16[1024,1024]{1,0:T(8,128)(2,1)}, u32[]{:S(2)}) copy-start(bf16[1024,1024]{1,0:T(8,128)(2,1)} %param.12) | copy-start | bytes 6291460
  6.5 33.1 %all-gather.3.cloned.1.call-start = ((), (), s32[]{:S(2)}) async-start(), calls=%async_computation | async-start | bytes 1310720 | tf_op jit(solution)/shard_map/all_gather | solution.py:50
  8.5 86.7 %all-gather.5.cloned.1.call-start = ((), (), s32[]{:S(2)}) async-start(), calls=%async_computation.1 | async-start | bytes 9437184 | tf_op jit(solution)/shard_map/all_gather | solution.py:51
  39.7 379.7 %all-reduce.4.cloned.1.call-start = ((), (), s32[]{:S(2)}) async-start(), calls=%async_computation.2 | async-start | bytes 262144 | tf_op jit(solution)/shard_map/pmax | solution.py:56
  39.8 67.9 %copy-start.4 = (s32[8]{0:T(128)S(1)}, s32[8]{0:T(128)}, u32[]{:S(2)}) copy-start(s32[8]{0:T(128)} %param.14) | copy-start | bytes 100
  115.8 3.2 copy-start.1
  139.1 3.2 copy-start.1
  162.5 3.2 copy-start.1
  185.8 3.2 copy-start.1
  209.2 3.2 copy-start.1
  232.6 3.2 copy-start.1
  256.0 3.2 copy-start.1
  279.3 3.2 copy-start.1
  294.6 418.6 %all-reduce.6.cloned.1.call-start = ((), (), s32[]{:S(2)}) async-start(), calls=%async_computation.3 | async-start | bytes 33816576 | tf_op jit(solution)/shard_map/psum | solution.py:69
  432.4 0.7 copy-start.3
  432.4 1.3 copy-start.2
Sparse Core Ops, SparseCore 0:
  8.9 30.6 all-gather.2
  41.5 53.6 all-gather.4
  294.7 124.6 all-reduce.3
  432.5 280.6 all-reduce.5
where the time goes:
time: 733 us; the launch traced here: 731 us
  waiting for transfers between devices  488 us (67%)
  local copies, waits for them, and re-layouts  126 us (17%)
  matrix products  65 us (9%)
  other arithmetic  38.3 us (5%)
  between operations  13.3 us (2%)
    psum x1, waiting for transfers between devices, body(): numer, total = lax.psum((weighted, mass), ('row', 'col'))  276 us
    pmax x1, waiting for transfers between devices, body(): peak_all = lax.pmax(peak_part, ('row', 'col'))  125 us
    dynamic_slice x48, local copies, waits for them, and re-layouts, cache_partials(): return lax.map(one_user, (whole, key_cache, value_cache, lengths))  57.9 us
    all_gather x1, waiting for transfers between devices, body(): whole = lax.all_gather(whole, 'row', axis=1, tiled=True)  55.4 us
    dot_general x8, matrix products, one_user(): jnp.einsum('kwgl,lkd->wkgd', weight.astype(jnp.bfloat16), v_heads, prefer...  39.7 us
    all_gather x1, waiting for transfers between devices, body(): whole = lax.all_gather(queries, 'col', axis=2, tiled=True)  31.1 us
    while x16, local copies, waits for them, and re-layouts  25.8 us
    dot_general x8, matrix products, one_user(): jnp.einsum('wkgd,lkd->kwgl', q_heads, k_heads, preferred_element_type=jnp...  22.7 us
  transfers between devices with their start and end apart: 4, of which 4 were waited for; matrix products, arithmetic and copies ran while one was open for 1% of the time, Pallas kernels for 0%

commit v1 on v0

--- a/solution.py
+++ b/solution.py
@@ -48,7 +48,12 @@
     row_at = lax.axis_index("row")
     col_at = lax.axis_index("col")
     whole = lax.all_gather(queries, "col", axis=2, tiled=True)
-    whole = lax.all_gather(whole, "row", axis=1, tiled=True)
+    ring = [whole]
+    for hop in range(7):
+        ring.append(lax.ppermute(ring[-1], "row", [(dev, (dev + 1) % 8) for dev in range(8)]))
+    whole = jnp.roll(
+        jnp.concatenate(ring[::-1], axis=1), (lax.axis_index("row") + 1) * ring[0].shape[1], axis=1
+    )
     offset = (row_at * lax.axis_size("col") + col_at) * key_cache.shape[1]
     numer_part, peak_part, total_part = cache_partials(
         whole, key_cache, value_cache, lengths, offset

time: 733 us -> 824 us (1.12)
  waiting for transfers between devices: 488 us -> 539 us
  local copies, waits for them, and re-layouts: 126 us -> 164 us
    ppermute x0 -> x7, waiting for transfers between devices: none -> 106 us  [body(): lax.ppermute(ring[-1], 'row', [(dev, (dev + 1) % 8) for dev in range(8)])]
    all_gather x1 -> x0, waiting for transfers between devices: 55.4 us -> none  [body(): whole = lax.all_gather(whole, 'row', axis=1, tiled=True)]
    unnamed x12 -> x48, local copies, waits for them, and re-layouts: 2.84 us -> 33.8 us
    while x17 -> x16, local copies, waits for them, and re-layouts: 38.3 us -> 25.9 us
    dynamic_slice x48 -> x56, local copies, waits for them, and re-layouts: 57.9 us -> 68.1 us  [cache_partials(): return lax.map(one_user, (whole, key_cache, value_cache, lengths))]
  transfers between devices with their start and end apart: 4 -> 10, of which waited for: 4 -> 10; matrix products, arithmetic and copies ran while one was open for 1% -> 0% of each run, Pallas kernels for 0% -> 0%
where the time goes in v1:
time: 824 us; the launch traced here: 822 us
  waiting for transfers between devices  539 us (65%)
  local copies, waits for them, and re-layouts  164 us (20%)
  matrix products  67.5 us (8%)
  other arithmetic  38.4 us (5%)
  between operations  13.3 us (2%)
    psum x1, waiting for transfers between devices, body(): numer, total = lax.psum((weighted, mass), ('row', 'col'))  276 us
    pmax x1, waiting for transfers between devices, body(): peak_all = lax.pmax(peak_part, ('row', 'col'))  123 us
    ppermute x7, waiting for transfers between devices, body(): lax.ppermute(ring[-1], 'row', [(dev, (dev + 1) % 8) for dev in range(8)])  106 us
    dynamic_slice x56, local copies, waits for them, and re-layouts, cache_partials(): return lax.map(one_user, (whole, key_cache, value_cache, lengths))  68.1 us
    dot_general x8, matrix products, one_user(): jnp.einsum('kwgl,lkd->wkgd', weight.astype(jnp.bfloat16), v_heads, prefer...  39.7 us
    unnamed x48, local copies, waits for them, and re-layouts  33.8 us
    all_gather x1, waiting for transfers between devices, body(): whole = lax.all_gather(queries, 'col', axis=2, tiled=True)  32.3 us
    while x16, local copies, waits for them, and re-layouts  25.9 us
  transfers between devices with their start and end apart: 10, of which 10 were waited for; matrix products, arithmetic and copies ran while one was open for 0% of the time, Pallas kernels for 0%

profile of v1, /device:TPU:0, one launch (start us, length us, event | category | flops | bytes accessed | tf_op | source)
XLA Modules:
  0.0 822.4 jit_solution(13502564973178384810)
XLA Ops:
  7.3 32.3 %all-gather.2.cloned.1.call-done = bf16[8,16,4096]{2,1,0:T(8,128)(2,1)} async-done(((bf16[8,16,1024]{2,1,0:T(8,128)(2,1)}), bf16[8,16,4096]{2,1,0:T(8,128)(2,1)}) %all-gather.2.cloned.1.call-update) | async-done | bytes 1048592 | tf_op jit(solution)/shard_map/all_gather | solution.py:50
  39.6 15.3 %collective-permute-done = bf16[8,16,4096]{2,1,0:T(8,128)(2,1)S(1)} collective-permute-done((bf16[8,16,4096]{2,1,0:T(8,128)(2,1)}, bf16[8,16,4096]{2,1,0:T(8,128)(2,1)S(1)}, u32[]{:S(2)}, u32[]{:S(2)}) %collective-permute-start) | collective-permute-done | bytes 1048608 | tf_op jit(solution)/shard_map/ppermute | solution.py:53
  56.0 15.1 %collective-permute-done.1 = bf16[8,16,4096]{2,1,0:T(8,128)(2,1)S(1)} collective-permute-done((bf16[8,16,4096]{2,1,0:T(8,128)(2,1)S(1)}, bf16[8,16,4096]{2,1,0:T(8,128)(2,1)S(1)}, u32[]{:S(2)}, u32[]{:S(2)}) %collective-permute-start.1) | collective-permute-done | bytes 1048608 | tf_op jit(solution)/shard_map/ppermute | solution.py:53
  72.1 15.1 %collective-permute-done.2 = bf16[8,16,4096]{2,1,0:T(8,128)(2,1)S(1)} collective-permute-done((bf16[8,16,4096]{2,1,0:T(8,128)(2,1)S(1)}, bf16[8,16,4096]{2,1,0:T(8,128)(2,1)S(1)}, u32[]{:S(2)}, u32[]{:S(2)}) %collective-permute-start.2) | collective-permute-done | bytes 1048608 | tf_op jit(solution)/shard_map/ppermute | solution.py:53
  88.2 15.1 %collective-permute-done.3 = bf16[8,16,4096]{2,1,0:T(8,128)(2,1)S(1)} collective-permute-done((bf16[8,16,4096]{2,1,0:T(8,128)(2,1)S(1)}, bf16[8,16,4096]{2,1,0:T(8,128)(2,1)S(1)}, u32[]{:S(2)}, u32[]{:S(2)}) %collective-permute-start.3) | collective-permute-done | bytes 1048608 | tf_op jit(solution)/shard_map/ppermute | solution.py:53
  104.3 15.1 %collective-permute-done.4 = bf16[8,16,4096]{2,1,0:T(8,128)(2,1)S(1)} collective-permute-done((bf16[8,16,4096]{2,1,0:T(8,128)(2,1)S(1)}, bf16[8,16,4096]{2,1,0:T(8,128)(2,1)S(1)}, u32[]{:S(2)}, u32[]{:S(2)}) %collective-permute-start.4) | collective-permute-done | bytes 1048608 | tf_op jit(solution)/shard_map/ppermute | solution.py:53
  120.4 15.2 %collective-permute-done.5 = bf16[8,16,4096]{2,1,0:T(8,128)(2,1)} collective-permute-done((bf16[8,16,4096]{2,1,0:T(8,128)(2,1)S(1)}, bf16[8,16,4096]{2,1,0:T(8,128)(2,1)}, u32[]{:S(2)}, u32[]{:S(2)}) %collective-permute-start.5) | collective-permute-done | bytes 1048608 | tf_op jit(solution)/shard_map/ppermute | solution.py:53
  135.7 15.4 %collective-permute-done.6 = bf16[8,16,4096]{2,1,0:T(8,128)(2,1)} collective-permute-done((bf16[8,16,4096]{2,1,0:T(8,128)(2,1)}, bf16[8,16,4096]{2,1,0:T(8,128)(2,1)}, u32[]{:S(2)}, u32[]{:S(2)}) %collective-permute-start.6) | collective-permute-done | bytes 1048608 | tf_op jit(solution)/shard_map/ppermute | solution.py:53
  180.1 7.7 constant_dynamic-slice_fusion.4
  187.8 199.8 %while.14 = (s32[]{:T(128)}, f32[8,128,4096]{1,2,0:T(8,128)}, f32[8,128,32]{1,2,0:T(8,128)}, f32[8,128,32]{1,2,0:T(8,128)S(1)}, bf16[8,512,1024]{2,1,0:T(8,128)(...) while((s32[]{:T(128)}, f32[8,128,4096]{1,2,0:T(8,128)}, ...), condition=%wide.region_3.4_spmd, body=%wide.region_0.3_spmd.sunk | while | flops 1100997632 | bytes 80874656 | solution.py:41
  194.3 3.2 fusion.35
  197.5 3.2 copy-done.1
  206.3 5.0 fusion.36
  222.5 3.2 copy-done.1
  231.3 5.0 fusion.36
  244.2 3.2 fusion.35
  247.4 3.2 copy-done.1
  256.3 5.0 fusion.36
  272.4 3.2 copy-done.1
  281.2 5.0 fusion.36
  297.4 3.2 copy-done.1
  306.3 5.0 fusion.36
  322.4 3.2 copy-done.1
  331.3 5.0 fusion.36
  347.4 3.2 copy-done.1
  356.3 5.0 fusion.36
  372.4 3.2 copy-done.1
  381.2 5.0 fusion.36
  387.9 123.0 %all-reduce.4.cloned.1.call-done = f32[8,128,32]{1,2,0:T(8,128)} async-done(((f32[8,128,32]{1,2,0:T(8,128)}), f32[8,128,32]{1,2,0:T(8,128)}) %all-reduce.4.cloned.1.call-update) | async-done | bytes 131088 | tf_op jit(solution)/shard_map/pmax | solution.py:61
  512.5 11.3 %bitcast_multiply_fusion = f32[8,128,4096]{1,2,0:T(8,128)} fusion(f32[8,128,4096]{1,2,0:T(8,128)} %get-tuple-element.54, f32[8,128,32]{1,2,0:T(8,128)S(1)} %get-tuple-element.117), kind=kLoop, calls=%fused_computation.17 | loop fusion | flops 4194304 | bytes 33685504 | tf_op jit(solution)/shard_map/mul | solution.py:63
  528.3 276.3 %all-reduce.6.cloned.1.call-done = (f32[8,128,4096]{1,2,0:T(8,128)}, f32[8,128,32]{1,2,0:T(8,128)}) async-done(((f32[8,128,4096]{1,2,0:T(8,128)}, f32[8,128,32]{1,2,0:T(8,128)}), (f32[8,128,4096]{1,2,0:T(8,128)}, f32[8,128,32]{1,2,0:T(8,128)})) %all-reduce.6.cloned.1.call-update) | async-done | bytes 16908304 | tf_op jit(solution)/shard_map/psum | solution.py:74
  805.8 5.3 constant_dynamic-slice_fusion.3
  (181 shorter events, 174.5 us)
Async XLA Ops:
  6.5 517.3 %copy-start = (bf16[1024,1024]{1,0:T(8,128)(2,1)S(1)}, bf16[1024,1024]{1,0:T(8,128)(2,1)}, u32[]{:S(2)}) copy-start(bf16[1024,1024]{1,0:T(8,128)(2,1)} %param.12) | copy-start | bytes 6291460
  6.5 33.1 %all-gather.2.cloned.1.call-start = ((), (), s32[]{:S(2)}) async-start(), calls=%async_computation | async-start | bytes 1310720 | tf_op jit(solution)/shard_map/all_gather | solution.py:50
  7.3 503.6 %all-reduce.4.cloned.1.call-start = ((), (), s32[]{:S(2)}) async-start(), calls=%async_computation.1 | async-start | bytes 262144 | tf_op jit(solution)/shard_map/pmax | solution.py:61
  39.6 139.4 %copy-start.2 = (bf16[8,16,4096]{2,1,0:T(8,128)(2,1)S(1)}, bf16[8,16,4096]{2,1,0:T(8,128)(2,1)}, u32[]{:S(2)}) copy-start(bf16[8,16,4096]{2,1,0:T(8,128)(2,1)} %all-gather.2.cloned.1.call-done) | copy-start | bytes 3145732
  39.6 15.3 %collective-permute-start = (bf16[8,16,4096]{2,1,0:T(8,128)(2,1)}, bf16[8,16,4096]{2,1,0:T(8,128)(2,1)S(1)}, u32[]{:S(2)}, u32[]{:S(2)}) collective-permute-start(bf16[8,16,4096]{2,1,0:T(8,128)(2,1)} %all-gather.2.cloned.1.call-done), channel_id=1, source_target_pairs={{0,4},{4,8},{8,12},{12,16},{16,20},{20,24},{24,28},{28,0},{1,5},{5... | collective-permute-start | bytes 3145736 | tf_op jit(solution)/shard_map/ppermute | solution.py:53
  55.0 1.0 copy-start.3
  56.0 15.1 %collective-permute-start.1 = (bf16[8,16,4096]{2,1,0:T(8,128)(2,1)S(1)}, bf16[8,16,4096]{2,1,0:T(8,128)(2,1)S(1)}, u32[]{:S(2)}, u32[]{:S(2)}) collective-permute-start(bf16[8,16,4096]{2,1,0:T(8,128)(2,1)S(1)} %collective-permute-done), channel_id=1, source_target_pairs={{0,4},{4,8},{8,12},{12,16},{16,20},{20,24},{24,28},{28,0},{1,5},{5... | collective-permute-start | bytes 3145736 | tf_op jit(solution)/shard_map/ppermute | solution.py:53
  71.1 1.0 copy-start.5
  72.1 15.1 %collective-permute-start.2 = (bf16[8,16,4096]{2,1,0:T(8,128)(2,1)S(1)}, bf16[8,16,4096]{2,1,0:T(8,128)(2,1)S(1)}, u32[]{:S(2)}, u32[]{:S(2)}) collective-permute-start(bf16[8,16,4096]{2,1,0:T(8,128)(2,1)S(1)} %collective-permute-done.1), channel_id=1, source_target_pairs={{0,4},{4,8},{8,12},{12,16},{16,20},{20,24},{24,28},{28,0},{1,5},{5... | collective-permute-start | bytes 3145736 | tf_op jit(solution)/shard_map/ppermute | solution.py:53
  87.2 1.0 copy-start.7
  88.2 15.1 %collective-permute-start.3 = (bf16[8,16,4096]{2,1,0:T(8,128)(2,1)S(1)}, bf16[8,16,4096]{2,1,0:T(8,128)(2,1)S(1)}, u32[]{:S(2)}, u32[]{:S(2)}) collective-permute-start(bf16[8,16,4096]{2,1,0:T(8,128)(2,1)S(1)} %collective-permute-done.2), channel_id=1, source_target_pairs={{0,4},{4,8},{8,12},{12,16},{16,20},{20,24},{24,28},{28,0},{1,5},{5... | collective-permute-start | bytes 3145736 | tf_op jit(solution)/shard_map/ppermute | solution.py:53
  103.3 1.0 copy-start.9
  104.3 15.1 %collective-permute-start.4 = (bf16[8,16,4096]{2,1,0:T(8,128)(2,1)S(1)}, bf16[8,16,4096]{2,1,0:T(8,128)(2,1)S(1)}, u32[]{:S(2)}, u32[]{:S(2)}) collective-permute-start(bf16[8,16,4096]{2,1,0:T(8,128)(2,1)S(1)} %collective-permute-done.3), channel_id=1, source_target_pairs={{0,4},{4,8},{8,12},{12,16},{16,20},{20,24},{24,28},{28,0},{1,5},{5... | collective-permute-start | bytes 3145736 | tf_op jit(solution)/shard_map/ppermute | solution.py:53
  119.5 1.0 copy-start.11
  120.4 15.2 %collective-permute-start.5 = (bf16[8,16,4096]{2,1,0:T(8,128)(2,1)S(1)}, bf16[8,16,4096]{2,1,0:T(8,128)(2,1)}, u32[]{:S(2)}, u32[]{:S(2)}) collective-permute-start(bf16[8,16,4096]{2,1,0:T(8,128)(2,1)S(1)} %collective-permute-done.4), channel_id=1, source_target_pairs={{0,4},{4,8},{8,12},{12,16},{16,20},{20,24},{24,28},{28,0},{1,5},{5... | collective-permute-start | bytes 3145736 | tf_op jit(solution)/shard_map/ppermute | solution.py:53
  135.6 15.4 %collective-permute-start.6 = (bf16[8,16,4096]{2,1,0:T(8,128)(2,1)}, bf16[8,16,4096]{2,1,0:T(8,128)(2,1)}, u32[]{:S(2)}, u32[]{:S(2)}) collective-permute-start(bf16[8,16,4096]{2,1,0:T(8,128)(2,1)} %collective-permute-done.5), channel_id=1, source_target_pairs={{0,4},{4,8},{8,12},{12,16},{16,20},{20,24},{24,28},{28,0},{1,5},{5... | collective-permute-start | bytes 3145736 | tf_op jit(solution)/shard_map/ppermute | solution.py:53
  135.6 38.2 %copy-start.12 = (bf16[8,16,4096]{2,1,0:T(8,128)(2,1)S(1)}, bf16[8,16,4096]{2,1,0:T(8,128)(2,1)}, u32[]{:S(2)}) copy-start(bf16[8,16,4096]{2,1,0:T(8,128)(2,1)} %copy-done.11) | copy-start | bytes 3145732
  135.7 39.2 %copy-start.10 = (bf16[8,16,4096]{2,1,0:T(8,128)(2,1)S(1)}, bf16[8,16,4096]{2,1,0:T(8,128)(2,1)}, u32[]{:S(2)}) copy-start(bf16[8,16,4096]{2,1,0:T(8,128)(2,1)} %copy-done.9) | copy-start | bytes 3145732
  135.7 40.2 %copy-start.8 = (bf16[8,16,4096]{2,1,0:T(8,128)(2,1)S(1)}, bf16[8,16,4096]{2,1,0:T(8,128)(2,1)}, u32[]{:S(2)}) copy-start(bf16[8,16,4096]{2,1,0:T(8,128)(2,1)} %copy-done.7) | copy-start | bytes 3145732
  135.7 41.2 %copy-start.6 = (bf16[8,16,4096]{2,1,0:T(8,128)(2,1)S(1)}, bf16[8,16,4096]{2,1,0:T(8,128)(2,1)}, u32[]{:S(2)}) copy-start(bf16[8,16,4096]{2,1,0:T(8,128)(2,1)} %copy-done.5) | copy-start | bytes 3145732
  135.7 42.3 %copy-start.4 = (bf16[8,16,4096]{2,1,0:T(8,128)(2,1)S(1)}, bf16[8,16,4096]{2,1,0:T(8,128)(2,1)}, u32[]{:S(2)}) copy-start(bf16[8,16,4096]{2,1,0:T(8,128)(2,1)} %copy-done.3) | copy-start | bytes 3145732
  169.3 18.6 %copy-start.15 = (s32[8]{0:T(128)S(1)}, s32[8]{0:T(128)}, u32[]{:S(2)}) copy-start(s32[8]{0:T(128)} %param.14) | copy-start | bytes 100
  197.5 3.3 copy-start.1
  222.5 3.3 copy-start.1
  247.4 3.3 copy-start.1
  272.4 3.3 copy-start.1
  297.4 3.3 copy-start.1
  322.4 3.3 copy-start.1
  347.4 3.3 copy-start.1
  372.4 3.3 copy-start.1
  387.7 416.9 %all-reduce.6.cloned.1.call-start = ((), (), s32[]{:S(2)}) async-start(), calls=%async_computation.2 | async-start | bytes 33816576 | tf_op jit(solution)/shard_map/psum | solution.py:74
  523.8 1.3 copy-start.13
  (1 other events, 0.7 us)
Sparse Core Ops, SparseCore 0:
  8.9 30.6 all-gather.1
  387.8 123.0 all-reduce.3
  524.0 280.6 all-reduce.5
